TPU v7x, 32 devices: a whole 2x2x4 slice. The times are simulated.
32 devices in a mesh: row: 4 (over y, x), col: 8 (over z, core).
Axes of the slice: x: 2, y: 2, z: 4, core: 2. Of those that a mesh axis runs over, the one named last changes fastest.
Arguments:
- pair_rep: bfloat16 [512, 512, 128], P('row', 'col'), may hold values from -6 to 6
- ln_gain: float32 [128], replicated, may hold values from 0.1 to 1.9
- ln_shift: float32 [128], replicated, may hold values from -3 to 3
- w_proj: bfloat16 [128, 512], replicated, may hold values from -0.5 to 0.5
- gate_bias: float32 [128], replicated, may hold values from -4 to 4
- w_bias: bfloat16 [128, 4], replicated, may hold values from -11 to 11
- w_out: bfloat16 [128, 128], replicated, may hold values from -0.5 to 0.5
- out_bias: float32 [128], replicated, may hold values from -3 to 3
- block_valid: int32 [4], replicated, may hold values from 0 to 1, as said below
Outputs:
- pair_out: bfloat16 [512, 512, 128], P('row', 'col')
Inputs may be any that keep to these rules, and one draw needn't show every extreme that they name: block_valid[b] is 1 when residues b * 128 to (b + 1) * 128 - 1 are present and 0 when they are padding; blocks 0 and 2 are always present, and at least one other block is always padding.
All inputs are finite; a program needn't handle non-finite values.
Results may differ from a plain program's by a relative error of at most 0.0082.
Values may be sent and summed in bfloat16 or wider, within the bound.
No kernel may reach another device: no remote copies, remote signals or barrier semaphores. Data moves between devices by JAX's collectives and lax.ppermute only.
A program may use at most 192 MiB of HBM per device.

v0:
```python
import math
import jax
import jax.numpy as jnp
from jax import lax
from jax.sharding import PartitionSpec as P

H = 4
HD = 32
BLK = 128


def layer_norm(values, ln_gain, ln_shift):
    widened = values.astype(jnp.float32)
    average = jnp.mean(widened, axis=-1, keepdims=True)
    spread = jnp.mean((widened - average) ** 2, axis=-1, keepdims=True)
    return ((widened - average) * lax.rsqrt(spread + 1e-05) * ln_gain + ln_shift).astype(
        jnp.bfloat16
    )


def residue_valid(block_valid, residues):
    blocks = block_valid.shape[0]
    block_width = residues // blocks
    owner = jnp.arange(residues, dtype=jnp.int32) // block_width
    matches = (owner[:, None] == jnp.arange(blocks, dtype=jnp.int32)[None, :]).astype(jnp.float32)
    return jnp.sum(matches * block_valid.astype(jnp.float32)[None, :], axis=1)


def start_state(width_j, query_count):
    running_max = jnp.full((H, width_j, query_count), -1e30, jnp.float32)
    denominator = jnp.zeros((H, width_j, query_count), jnp.float32)
    weighted = jnp.zeros((query_count, width_j, H, HD), jnp.float32)
    return (running_max, denominator, weighted)


def finish(carried):
    running_max, denominator, weighted = carried
    mixed = weighted / jnp.transpose(denominator, (2, 1, 0))[..., None]
    return mixed.reshape(mixed.shape[0], mixed.shape[1], H * HD).astype(jnp.bfloat16)


def fold_keys(carried, queries, key_rows, values, bias_part, validity):
    query_count, width_j, inner = queries.shape
    key_count = key_rows.shape[0]
    key_step = math.gcd(key_count, BLK)
    steps = key_count // key_step
    query_heads = queries.reshape(query_count, width_j, H, HD)
    key_blocks = key_rows.reshape(steps, key_step, width_j, H, HD)
    value_blocks = values.reshape(steps, key_step, width_j, H, HD)
    bias_blocks = jnp.transpose(bias_part.reshape(H, query_count, steps, key_step), (2, 0, 1, 3))
    mask_blocks = validity.reshape(steps, key_step)

    def update(carried_in, operands):
        key_part, value_part, bias_block, mask_part = operands
        running_max, denominator, weighted = carried_in
        scores = jnp.einsum(
            "ijhd,kjhd->hjik", query_heads, key_part, preferred_element_type=jnp.float32
        )
        scores = scores + bias_block[:, None, :, :]
        scores = jnp.where(mask_part[None, None, None, :] > 0, scores, jnp.float32(-1e30))
        renewed = jnp.maximum(running_max, jnp.max(scores, axis=-1))
        weights = jnp.exp(scores - renewed[..., None]) * mask_part[None, None, None, :]
        shrink = jnp.exp(running_max - renewed)
        denominator = denominator * shrink + jnp.sum(weights, axis=-1)
        product = jnp.einsum(
            "hjik,kjhd->ijhd",
            weights.astype(jnp.bfloat16),
            value_part,
            preferred_element_type=jnp.float32,
        )
        weighted = weighted * jnp.transpose(shrink, (2, 1, 0))[..., None] + product
        return (renewed, denominator, weighted)

    def scan_step(carried_in, operands):
        renewed = lax.cond(
            jnp.max(operands[3]) > 0, update, lambda kept, ignored: kept, carried_in, operands
        )
        return (renewed, None)

    result, ignored = lax.scan(
        scan_step, carried, (key_blocks, value_blocks, bias_blocks, mask_blocks)
    )
    return result


def shards(pair_rep, ln_gain, ln_shift, w_proj, gate_bias, w_bias, w_out, out_bias, block_valid):
    rows_dev, cols_dev, channels = pair_rep.shape
    row_count = lax.axis_size("row")
    row_id = lax.axis_index("row")
    col_id = lax.axis_index("col")
    residues = rows_dev * row_count
    inner = H * HD
    query_scale = HD ** (-0.5)
    validity = residue_valid(block_valid, residues)
    normed = layer_norm(pair_rep, ln_gain, ln_shift)
    flat_rows = normed.reshape(rows_dev * cols_dev, channels)
    bias_local = jnp.dot(flat_rows, w_bias, preferred_element_type=jnp.float32)
    bias_local = jnp.transpose(bias_local.reshape(rows_dev, cols_dev, H), (2, 1, 0))
    bias_cols = lax.all_gather(bias_local, "row", axis=2, tiled=True)
    regrouped = lax.all_to_all(normed, "row", split_axis=1, concat_axis=0, tiled=True)
    width_j = regrouped.shape[1]
    projected = jnp.dot(
        regrouped.reshape(residues * width_j, channels),
        w_proj[:, : 3 * inner],
        preferred_element_type=jnp.float32,
    )
    projected = projected.reshape(residues, width_j, 3 * inner)
    queries = (projected[..., :inner] * query_scale).astype(jnp.bfloat16)
    key_rows = projected[..., inner : 2 * inner].astype(jnp.bfloat16)
    values = projected[..., 2 * inner :].astype(jnp.bfloat16)
    bias_piece = lax.all_gather(bias_cols, "col", axis=1, tiled=True)
    span_rows = bias_piece.shape[1]
    query_block = math.gcd(span_rows, cols_dev)
    block_count = span_rows // query_block
    query_rows = queries
    query_rows = query_rows.reshape(block_count, query_block, width_j, inner)
    bias_blocks = jnp.transpose(
        bias_piece.reshape(H, block_count, query_block, residues), (1, 0, 2, 3)
    )

    def one_block(operands):
        query_part, bias_part = operands
        carried = fold_keys(
            start_state(width_j, query_block), query_part, key_rows, values, bias_part, validity
        )
        return finish(carried)

    results = lax.map(one_block, (query_rows, bias_blocks))
    gathered = results.reshape(span_rows, width_j, inner)
    attended = lax.all_to_all(gathered, "row", split_axis=0, concat_axis=1, tiled=True)
    gate_pre = jnp.dot(flat_rows, w_proj[:, 3 * inner :], preferred_element_type=jnp.float32)
    gate_pre = gate_pre.reshape(rows_dev, cols_dev, inner)
    gate_act = jax.nn.sigmoid(gate_pre + gate_bias)
    gated_rows = (gate_act * attended.astype(jnp.float32)).astype(jnp.bfloat16)
    update = jnp.dot(
        gated_rows.reshape(rows_dev * cols_dev, inner), w_out, preferred_element_type=jnp.float32
    )
    update = update.reshape(rows_dev, cols_dev, channels) + out_bias
    row_valid = lax.dynamic_slice_in_dim(validity, row_id * rows_dev, rows_dev, 0)
    col_valid = lax.dynamic_slice_in_dim(validity, col_id * cols_dev, cols_dev, 0)
    pair_mask = row_valid[:, None] * col_valid[None, :]
    return (pair_rep.astype(jnp.float32) + update * pair_mask[..., None]).astype(jnp.bfloat16)


def solution(mesh):
    return jax.shard_map(
        shards,
        mesh=mesh,
        in_specs=(P("row", "col", None), P(), P(), P(), P(), P(), P(), P(), P()),
        out_specs=P("row", "col", None),
        check_vma=False,
    )
```

profile of v0, /device:TPU:0, one launch (start us, length us, event | category | flops | bytes accessed | tf_op | source)
XLA Modules:
  0.0 358.7 jit_solution(1915389312735172597)
XLA Ops:
  10.1 6.1 %fusion.16 = f32[128,64]{0,1:T(8,128)S(1)} fusion(f32[128,64]{0,1:T(8,128)S(1)} %broadcast_multiply_fusion.1, bf16[128,64,128]{2,1,0:T(8,128)(2,1)S(1)} %copy-done.1), kind=kLoop, calls=%fused_computation.31 | loop fusion | flops 4186112 | bytes 2162688 | tf_op jit(solution)/shard_map/reduce_sum | solution.py:15
  23.2 12.3 %all_gather.6 = f32[4,64,512]{2,0,1:T(4,128)} all-gather(f32[4,64,128]{2,0,1:T(4,128)S(1)} %convolution_bitcast_fusion.1), channel_id=1, replica_groups=mesh['row'=4,'col'=8] {'row'}, dimensions={2}, use_global_device_ids=true | all-gather | bytes 655360 | tf_op jit(solution)/shard_map/all_gather | solution.py:99
  39.4 23.1 %all-to-all-done = bf16[128,64,128]{2,0,1:T(8,128)(2,1)S(1)} async-done(((bf16[128,64,128]{2,0,1:T(8,128)(2,1)}), bf16[128,64,128]{2,0,1:T(8,128)(2,1)S(1)}, u32[]{:S(2)}, u32[]{:S(2)}) %all-to-all-start) | async-done | bytes 2097184 | tf_op jit(solution)/shard_map/all_to_all | solution.py:100
  63.4 6.3 %fusion.38 = (bf16[512,16,384]{2,0,1:T(8,128)(2,1)S(1)}, f32[512,16,384]{2,0,1:T(8,128)}) fusion(bf16[512,16,128]{2,0,1:T(8,128)(2,1)S(1)} %bitcast.98, bf16[128,512]{1,0:T(8,128)(2,1)S(1)} %copy-done.5), kind=kOutput, calls=%fused_computation.65 | convolution fusion | flops 808452096 | bytes 21069824 | tf_op jit(solution)/shard_map/dot_general | solution.py:102
  90.2 5.4 %copy.101 = f32[4,8,64,512]{3,2,0,1:T(8,128)} copy(f32[4,8,64,512]{3,0,2,1:T(4,128)} %bitcast.100) | data formatting | bytes 8388608 | tf_op jit(solution)/shard_map/reshape | solution.py:118
  95.6 212.3 %while.27 = (s32[]{:T(128)}, bf16[8,64,16,128]{3,2,1,0:T(8,128)(2,1)}, bf16[512,16,128]{0,2,1:T(8,128)(2,1)}, bf16[512,16,128]{0,2,1:T(8,128)(2,1)}, f32[8,4,64,...) while((s32[]{:T(128)}, ...), condition=%wide.wide.region_11.12_spmd, body=%wide.wide.region_3.11_spmd.sunk | while | flops 72364288 | bytes 25006472 | solution.py:128
  105.2 15.8 %while.28 = (s32[]{:T(128)}, f32[4,16,64]{2,1,0:T(8,128)S(1)}, f32[4,16,64]{2,1,0:T(8,128)S(1)}, f32[64,16,4,32]{0,3,2,1:T(8,128)S(1)}, f32[4,128]{1,0:T(4,128)S...) while((s32[]{:T(128)}, f32[4,16,64]{2,1,0:T(8,128)S(1)}, ...), condition=%wide.region_10.10_spmd, body=%wide.region_4.9_spmd.sunk | while | flops 72102144 | bytes 9457287 | solution.py:80
  131.7 15.8 %while.28 = (s32[]{:T(128)}, f32[4,16,64]{2,1,0:T(8,128)S(1)}, f32[4,16,64]{2,1,0:T(8,128)S(1)}, f32[64,16,4,32]{0,3,2,1:T(8,128)S(1)}, f32[4,128]{1,0:T(4,128)S...) while((s32[]{:T(128)}, f32[4,16,64]{2,1,0:T(8,128)S(1)}, ...), condition=%wide.region_10.10_spmd, body=%wide.region_4.9_spmd.sunk | while | flops 72102144 | bytes 9457287 | solution.py:80
  133.1 5.2 %conditional.2 = ((f32[4,16,64]{2,1,0:T(8,128)S(1)}, f32[4,16,64]{2,1,0:T(8,128)S(1)}, f32[64,16,4,32]{0,3,2,1:T(8,128)S(1)})) conditional(s32[]{:T(128)} %convert_element_type.97, (f32[4,16,64]{2,1,0:T(8,128)S(1)}, f32[4,16,64]{2,1,0:T(8,128)S(1)}, f32[64,16,4,32]{0,3,2,1:T(8,128)S(1)}) %tuple.69, (f32[1,128]{1,0:T(1,128)S(1)}, ...), branch_computations={%region_6.5_spmd, %region_7.8_spmd} | conditional | flops 72102016 | bytes 9456036 | solution.py:75
  140.9 5.2 %conditional.2 = ((f32[4,16,64]{2,1,0:T(8,128)S(1)}, f32[4,16,64]{2,1,0:T(8,128)S(1)}, f32[64,16,4,32]{0,3,2,1:T(8,128)S(1)})) conditional(s32[]{:T(128)} %convert_element_type.97, (f32[4,16,64]{2,1,0:T(8,128)S(1)}, f32[4,16,64]{2,1,0:T(8,128)S(1)}, f32[64,16,4,32]{0,3,2,1:T(8,128)S(1)}) %tuple.69, (f32[1,128]{1,0:T(1,128)S(1)}, ...), branch_computations={%region_6.5_spmd, %region_7.8_spmd} | conditional | flops 72102016 | bytes 9456036 | solution.py:75
  158.3 15.8 %while.28 = (s32[]{:T(128)}, f32[4,16,64]{2,1,0:T(8,128)S(1)}, f32[4,16,64]{2,1,0:T(8,128)S(1)}, f32[64,16,4,32]{0,3,2,1:T(8,128)S(1)}, f32[4,128]{1,0:T(4,128)S...) while((s32[]{:T(128)}, f32[4,16,64]{2,1,0:T(8,128)S(1)}, ...), condition=%wide.region_10.10_spmd, body=%wide.region_4.9_spmd.sunk | while | flops 72102144 | bytes 9457287 | solution.py:80
  184.8 15.8 %while.28 = (s32[]{:T(128)}, f32[4,16,64]{2,1,0:T(8,128)S(1)}, f32[4,16,64]{2,1,0:T(8,128)S(1)}, f32[64,16,4,32]{0,3,2,1:T(8,128)S(1)}, f32[4,128]{1,0:T(4,128)S...) while((s32[]{:T(128)}, f32[4,16,64]{2,1,0:T(8,128)S(1)}, ...), condition=%wide.region_10.10_spmd, body=%wide.region_4.9_spmd.sunk | while | flops 72102144 | bytes 9457287 | solution.py:80
  211.3 15.8 %while.28 = (s32[]{:T(128)}, f32[4,16,64]{2,1,0:T(8,128)S(1)}, f32[4,16,64]{2,1,0:T(8,128)S(1)}, f32[64,16,4,32]{0,3,2,1:T(8,128)S(1)}, f32[4,128]{1,0:T(4,128)S...) while((s32[]{:T(128)}, f32[4,16,64]{2,1,0:T(8,128)S(1)}, ...), condition=%wide.region_10.10_spmd, body=%wide.region_4.9_spmd.sunk | while | flops 72102144 | bytes 9457287 | solution.py:80
  212.7 5.2 %conditional.2 = ((f32[4,16,64]{2,1,0:T(8,128)S(1)}, f32[4,16,64]{2,1,0:T(8,128)S(1)}, f32[64,16,4,32]{0,3,2,1:T(8,128)S(1)})) conditional(s32[]{:T(128)} %convert_element_type.97, (f32[4,16,64]{2,1,0:T(8,128)S(1)}, f32[4,16,64]{2,1,0:T(8,128)S(1)}, f32[64,16,4,32]{0,3,2,1:T(8,128)S(1)}) %tuple.69, (f32[1,128]{1,0:T(1,128)S(1)}, ...), branch_computations={%region_6.5_spmd, %region_7.8_spmd} | conditional | flops 72102016 | bytes 9456036 | solution.py:75
  220.6 5.2 %conditional.2 = ((f32[4,16,64]{2,1,0:T(8,128)S(1)}, f32[4,16,64]{2,1,0:T(8,128)S(1)}, f32[64,16,4,32]{0,3,2,1:T(8,128)S(1)})) conditional(s32[]{:T(128)} %convert_element_type.97, (f32[4,16,64]{2,1,0:T(8,128)S(1)}, f32[4,16,64]{2,1,0:T(8,128)S(1)}, f32[64,16,4,32]{0,3,2,1:T(8,128)S(1)}) %tuple.69, (f32[1,128]{1,0:T(1,128)S(1)}, ...), branch_computations={%region_6.5_spmd, %region_7.8_spmd} | conditional | flops 72102016 | bytes 9456036 | solution.py:75
  237.9 15.8 %while.28 = (s32[]{:T(128)}, f32[4,16,64]{2,1,0:T(8,128)S(1)}, f32[4,16,64]{2,1,0:T(8,128)S(1)}, f32[64,16,4,32]{0,3,2,1:T(8,128)S(1)}, f32[4,128]{1,0:T(4,128)S...) while((s32[]{:T(128)}, f32[4,16,64]{2,1,0:T(8,128)S(1)}, ...), condition=%wide.region_10.10_spmd, body=%wide.region_4.9_spmd.sunk | while | flops 72102144 | bytes 9457287 | solution.py:80
  239.2 5.2 %conditional.2 = ((f32[4,16,64]{2,1,0:T(8,128)S(1)}, f32[4,16,64]{2,1,0:T(8,128)S(1)}, f32[64,16,4,32]{0,3,2,1:T(8,128)S(1)})) conditional(s32[]{:T(128)} %convert_element_type.97, (f32[4,16,64]{2,1,0:T(8,128)S(1)}, f32[4,16,64]{2,1,0:T(8,128)S(1)}, f32[64,16,4,32]{0,3,2,1:T(8,128)S(1)}) %tuple.69, (f32[1,128]{1,0:T(1,128)S(1)}, ...), branch_computations={%region_6.5_spmd, %region_7.8_spmd} | conditional | flops 72102016 | bytes 9456036 | solution.py:75
  247.1 5.2 %conditional.2 = ((f32[4,16,64]{2,1,0:T(8,128)S(1)}, f32[4,16,64]{2,1,0:T(8,128)S(1)}, f32[64,16,4,32]{0,3,2,1:T(8,128)S(1)})) conditional(s32[]{:T(128)} %convert_element_type.97, (f32[4,16,64]{2,1,0:T(8,128)S(1)}, f32[4,16,64]{2,1,0:T(8,128)S(1)}, f32[64,16,4,32]{0,3,2,1:T(8,128)S(1)}) %tuple.69, (f32[1,128]{1,0:T(1,128)S(1)}, ...), branch_computations={%region_6.5_spmd, %region_7.8_spmd} | conditional | flops 72102016 | bytes 9456036 | solution.py:75
  264.4 15.8 %while.28 = (s32[]{:T(128)}, f32[4,16,64]{2,1,0:T(8,128)S(1)}, f32[4,16,64]{2,1,0:T(8,128)S(1)}, f32[64,16,4,32]{0,3,2,1:T(8,128)S(1)}, f32[4,128]{1,0:T(4,128)S...) while((s32[]{:T(128)}, f32[4,16,64]{2,1,0:T(8,128)S(1)}, ...), condition=%wide.region_10.10_spmd, body=%wide.region_4.9_spmd.sunk | while | flops 72102144 | bytes 9457287 | solution.py:80
  265.8 5.2 %conditional.2 = ((f32[4,16,64]{2,1,0:T(8,128)S(1)}, f32[4,16,64]{2,1,0:T(8,128)S(1)}, f32[64,16,4,32]{0,3,2,1:T(8,128)S(1)})) conditional(s32[]{:T(128)} %convert_element_type.97, (f32[4,16,64]{2,1,0:T(8,128)S(1)}, f32[4,16,64]{2,1,0:T(8,128)S(1)}, f32[64,16,4,32]{0,3,2,1:T(8,128)S(1)}) %tuple.69, (f32[1,128]{1,0:T(1,128)S(1)}, ...), branch_computations={%region_6.5_spmd, %region_7.8_spmd} | conditional | flops 72102016 | bytes 9456036 | solution.py:75
  273.6 5.2 %conditional.2 = ((f32[4,16,64]{2,1,0:T(8,128)S(1)}, f32[4,16,64]{2,1,0:T(8,128)S(1)}, f32[64,16,4,32]{0,3,2,1:T(8,128)S(1)})) conditional(s32[]{:T(128)} %convert_element_type.97, (f32[4,16,64]{2,1,0:T(8,128)S(1)}, f32[4,16,64]{2,1,0:T(8,128)S(1)}, f32[64,16,4,32]{0,3,2,1:T(8,128)S(1)}) %tuple.69, (f32[1,128]{1,0:T(1,128)S(1)}, ...), branch_computations={%region_6.5_spmd, %region_7.8_spmd} | conditional | flops 72102016 | bytes 9456036 | solution.py:75
  291.0 15.8 %while.28 = (s32[]{:T(128)}, f32[4,16,64]{2,1,0:T(8,128)S(1)}, f32[4,16,64]{2,1,0:T(8,128)S(1)}, f32[64,16,4,32]{0,3,2,1:T(8,128)S(1)}, f32[4,128]{1,0:T(4,128)S...) while((s32[]{:T(128)}, f32[4,16,64]{2,1,0:T(8,128)S(1)}, ...), condition=%wide.region_10.10_spmd, body=%wide.region_4.9_spmd.sunk | while | flops 72102144 | bytes 9457287 | solution.py:80
  312.0 24.0 %all-to-all-done.1 = bf16[512,16,128]{2,1,0:T(8,128)(2,1)S(1)} async-done(((bf16[512,16,128]{2,1,0:T(8,128)(2,1)}), bf16[512,16,128]{2,1,0:T(8,128)(2,1)S(1)}, u32[]{:S(2)}, u32[]{:S(2)}) %all-to-all-start.1) | async-done | bytes 2097184 | tf_op jit(solution)/shard_map/all_to_all | solution.py:130
  339.1 8.5 %fusion.20 = bf16[128,64,128]{2,0,1:T(8,128)(2,1)} fusion(f32[128,64]{0,1:T(8,128)S(1)} %broadcast_multiply_fusion, f32[128]{0:T(128)S(1)} %copy-done.10, bf16[128,64,128]{2,1,0:T(8,128)(2,1)S(1)} %copy-done.2, f32[128,64,128]{2,1,0:T(8,128)} %bitcast.101, bf16[128,64,128]{2,0,1:T(8,128)(2,1)} %copy-done.3, f32[128]{0:T(128)S(1)} %copy-done.11, ...), kind=kOutput, calls=%fused_computation.35 | convolution fusion | flops 548405248 | bytes 10585088 | tf_op jit(solution)/shard_map/dot_general | solution.py:135
  (371 shorter events, 277.5 us)
Async XLA Ops:
  6.5 332.5 %copy-start = (bf16[128,128]{1,0:T(8,128)(2,1)S(1)}, bf16[128,128]{1,0:T(8,128)(2,1)}, u32[]{:S(2)}) copy-start(bf16[128,128]{1,0:T(8,128)(2,1)} %param.21) | copy-start | bytes 98308
  6.5 3.6 copy-start.1
  6.5 9.7 %copy-start.8 = (f32[128]{0:T(128)S(1)}, f32[128]{0:T(128)}, u32[]{:S(2)}) copy-start(f32[128]{0:T(128)} %param.16) | copy-start | bytes 1540
  6.5 9.7 %copy-start.7 = (f32[128]{0:T(128)S(1)}, f32[128]{0:T(128)}, u32[]{:S(2)}) copy-start(f32[128]{0:T(128)} %param.17) | copy-start | bytes 1540
  6.5 83.7 %all-gather.2.cloned.1.call-start = ((), (), s32[]{:S(2)}) async-start(), calls=%async_computation.2 | async-start | bytes 4718592 | tf_op jit(solution)/shard_map/all_gather | solution.py:111
  16.3 6.3 %copy-start.6 = (bf16[128,4]{0,1:T(4,128)(2,1)S(1)}, bf16[128,4]{0,1:T(4,128)(2,1)}, u32[]{:S(2)}) copy-start(bf16[128,4]{0,1:T(4,128)(2,1)} %param.20) | copy-start | bytes 3076
  21.2 1.3 copy-start.3
  35.5 3.8 %copy-start.9 = (s32[4]{0:T(128)S(1)}, s32[4]{0:T(128)}, u32[]{:S(2)}) copy-start(s32[4]{0:T(128)} %param.23) | copy-start | bytes 52
  35.5 27.0 %all-to-all-start = ((bf16[128,64,128]{2,0,1:T(8,128)(2,1)}), bf16[128,64,128]{2,0,1:T(8,128)(2,1)S(1)}, u32[]{:S(2)}, u32[]{:S(2)}) async-start(bf16[128,64,128]{2,0,1:T(8,128)(2,1)} %copy-done.3), calls=%async_computation | async-start | bytes 4194304 | tf_op jit(solution)/shard_map/all_to_all | solution.py:100
  62.5 0.9 copy-start.5
  75.8 2.3 copy-start.4
  307.9 28.1 %all-to-all-start.1 = ((bf16[512,16,128]{2,1,0:T(8,128)(2,1)}), bf16[512,16,128]{2,1,0:T(8,128)(2,1)S(1)}, u32[]{:S(2)}, u32[]{:S(2)}) async-start(bf16[512,16,128]{2,1,0:T(8,128)(2,1)} %bitcast.102), calls=%async_computation.1 | async-start | bytes 4194304 | tf_op jit(solution)/shard_map/all_to_all | solution.py:130
  336.4 2.6 copy-start.2
  336.4 2.6 copy-start.10
  336.4 2.6 copy-start.11
Sparse Core Ops, SparseCore 0:
  35.6 47.1 all-gather.1
where the time goes:
time: 362 us; the launch traced here: 359 us
  local copies, waits for them, and re-layouts  116 us (32%)
  matrix products  74.5 us (21%)
  other arithmetic  64.1 us (18%)
  waiting for transfers between devices  47.1 us (13%)
  loops' own time  23.6 us (7%)
  between operations  13.6 us (4%)
  blocking collectives  12.3 us (3%)
  starting transfers between devices  7.66 us (2%)
    while x32, local copies, waits for them, and re-layouts, fold_keys(): lax.scan(scan_step, carried, (key_blocks, value_blocks, bias_blocks, mask...  55.1 us
    dot_general x16, matrix products, update(): jnp.einsum('ijhd,kjhd->hjik', query_heads, key_part, preferred_element_ty...  31.4 us
    dot_general x16, matrix products, update(): jnp.einsum('hjik,kjhd->ijhd', weights.astype(jnp.bfloat16), value_part, p...  27.6 us
    all_to_all x1, waiting for transfers between devices, shards(): lax.all_to_all(gathered, 'row', split_axis=0, concat_axis=1, tiled=True)  24 us
    all_to_all x1, waiting for transfers between devices, shards(): lax.all_to_all(normed, 'row', split_axis=1, concat_axis=0, tiled=True)  23.1 us
    reduce_max x32, other arithmetic, scan_step(): jnp.max(operands[3]) > 0  21.5 us
    convert_element_type x16, other arithmetic, update(): weights.astype(jnp.bfloat16)  21.5 us
    another operation x8, loops' own time, fold_keys(): lax.scan(scan_step, carried, (key_blocks, value_blocks, bias_blocks, mask...  21.4 us
  transfers between devices with their start and end apart: 3, of which 2 were waited for; matrix products, arithmetic and copies ran while one was open for 8% of the time, Pallas kernels for 0%

commit v1 on v0

--- a/solution.py
+++ b/solution.py
@@ -7,6 +7,29 @@
 H = 4
 HD = 32
 BLK = 128
+
+
+def cut_along(x, dim, size):
+    shape = x.shape
+    blocks = x.reshape(*shape[:dim], size, shape[dim] // size, *shape[dim + 1 :])
+    return jnp.moveaxis(blocks, dim, 0)
+
+
+def joined_along(blocks, dim):
+    lengths = list(blocks.shape[1:])
+    lengths[dim] *= blocks.shape[0]
+    return jnp.moveaxis(blocks, 0, dim).reshape(lengths)
+
+
+def exchange_in_pairs(x, axis, split_dim, concat_dim):
+    count, index = (lax.axis_size(axis), lax.axis_index(axis))
+    tiles = cut_along(x, split_dim, count)
+    finished = [tiles[index]]
+    for step in range(1, count):
+        sent = tiles[index ^ step]
+        finished.append(lax.ppermute(sent, axis, [(i, i ^ step) for i in range(count)]))
+    tiles = jnp.stack(finished)[index ^ jnp.arange(count)]
+    return joined_along(tiles, concat_dim)
 
 
 def layer_norm(values, ln_gain, ln_shift):
@@ -127,7 +150,7 @@
 
     results = lax.map(one_block, (query_rows, bias_blocks))
     gathered = results.reshape(span_rows, width_j, inner)
-    attended = lax.all_to_all(gathered, "row", split_axis=0, concat_axis=1, tiled=True)
+    attended = exchange_in_pairs(gathered, "row", 0, 1)
     gate_pre = jnp.dot(flat_rows, w_proj[:, 3 * inner :], preferred_element_type=jnp.float32)
     gate_pre = gate_pre.reshape(rows_dev, cols_dev, inner)
     gate_act = jax.nn.sigmoid(gate_pre + gate_bias)

time: 362 us -> 363 us (level)
    all_to_all x1 -> x0, waiting for transfers between devices: 24 us -> none  [shards(): lax.all_to_all(gathered, 'row', split_axis=0, concat_axis=1, tiled=True)]
    ppermute x0 -> x3, waiting for transfers between devices: none -> 20.6 us  [exchange_in_pairs(): lax.ppermute(sent, axis, [(i, i ^ step) for i in range(count)])]
    all_to_all x1 -> x0, starting transfers between devices: 3.83 us -> none  [shards(): lax.all_to_all(gathered, 'row', split_axis=0, concat_axis=1, tiled=True)]
  transfers between devices with their start and end apart: 3 -> 5, of which waited for: 2 -> 3; matrix products, arithmetic and copies ran while one was open for 8% -> 7% of each run, Pallas kernels for 0% -> 0%
where the time goes in v1:
time: 363 us; the launch traced here: 359 us
  local copies, waits for them, and re-layouts  118 us (33%)
  matrix products  74.7 us (21%)
  other arithmetic  66.7 us (18%)
  waiting for transfers between devices  43.7 us (12%)
  loops' own time  23.5 us (6%)
  between operations  13.6 us (4%)
  blocking collectives  12.3 us (3%)
  starting transfers between devices  7.38 us (2%)
    while x32, local copies, waits for them, and re-layouts, fold_keys(): lax.scan(scan_step, carried, (key_blocks, value_blocks, bias_blocks, mask...  55.3 us
    dot_general x16, matrix products, update(): jnp.einsum('ijhd,kjhd->hjik', query_heads, key_part, preferred_element_ty...  31.4 us
    dot_general x16, matrix products, update(): jnp.einsum('hjik,kjhd->ijhd', weights.astype(jnp.bfloat16), value_part, p...  27.6 us
    all_to_all x1, waiting for transfers between devices, shards(): lax.all_to_all(normed, 'row', split_axis=1, concat_axis=0, tiled=True)  23 us
    convert_element_type x16, other arithmetic, update(): weights.astype(jnp.bfloat16)  21.5 us
    reduce_max x32, other arithmetic, scan_step(): jnp.max(operands[3]) > 0  21.4 us
    another operation x8, loops' own time, fold_keys(): lax.scan(scan_step, carried, (key_blocks, value_blocks, bias_blocks, mask...  21.3 us
    ppermute x3, waiting for transfers between devices, exchange_in_pairs(): lax.ppermute(sent, axis, [(i, i ^ step) for i in range(count)])  20.6 us
  transfers between devices with their start and end apart: 5, of which 3 were waited for; matrix products, arithmetic and copies ran while one was open for 7% of the time, Pallas kernels for 0%

profile of v1, /device:TPU:0, one launch (start us, length us, event | category | flops | bytes accessed | tf_op | source)
XLA Modules:
  0.0 359.4 jit_solution(13729432276633699756)
XLA Ops:
  10.1 6.1 %fusion.16 = f32[128,64]{0,1:T(8,128)S(1)} fusion(f32[128,64]{0,1:T(8,128)S(1)} %broadcast_multiply_fusion.1, bf16[128,64,128]{2,1,0:T(8,128)(2,1)S(1)} %copy-done.1), kind=kLoop, calls=%fused_computation.32 | loop fusion | flops 4186112 | bytes 2162688 | tf_op jit(solution)/shard_map/reduce_sum | solution.py:38
  23.2 12.3 %all_gather.6 = f32[4,64,512]{2,0,1:T(4,128)} all-gather(f32[4,64,128]{2,0,1:T(4,128)S(1)} %convolution_bitcast_fusion.1), channel_id=1, replica_groups=mesh['row'=4,'col'=8] {'row'}, dimensions={2}, use_global_device_ids=true | all-gather | bytes 655360 | tf_op jit(solution)/shard_map/all_gather | solution.py:122
  39.5 23.0 %all-to-all-done = bf16[128,64,128]{2,0,1:T(8,128)(2,1)S(1)} async-done(((bf16[128,64,128]{2,0,1:T(8,128)(2,1)}), bf16[128,64,128]{2,0,1:T(8,128)(2,1)S(1)}, u32[]{:S(2)}, u32[]{:S(2)}) %all-to-all-start) | async-done | bytes 2097184 | tf_op jit(solution)/shard_map/all_to_all | solution.py:123
  63.4 6.3 %fusion.39 = (bf16[512,16,384]{2,0,1:T(8,128)(2,1)S(1)}, f32[512,16,384]{2,0,1:T(8,128)}) fusion(bf16[512,16,128]{2,0,1:T(8,128)(2,1)S(1)} %bitcast.106, bf16[128,512]{1,0:T(8,128)(2,1)S(1)} %copy-done.6), kind=kOutput, calls=%fused_computation.74 | convolution fusion | flops 808452096 | bytes 21069824 | tf_op jit(solution)/shard_map/dot_general | solution.py:125
  87.4 5.4 %copy.101 = f32[4,8,64,512]{3,2,0,1:T(8,128)} copy(f32[4,8,64,512]{3,0,2,1:T(4,128)} %bitcast.108) | data formatting | bytes 8388608 | tf_op jit(solution)/shard_map/reshape | solution.py:141
  92.8 212.3 %while.27 = (s32[]{:T(128)}, bf16[8,64,16,128]{3,2,1,0:T(8,128)(2,1)}, bf16[512,16,128]{0,2,1:T(8,128)(2,1)}, bf16[512,16,128]{0,2,1:T(8,128)(2,1)}, f32[8,4,64,...) while((s32[]{:T(128)}, ...), condition=%wide.wide.region_11.12_spmd, body=%wide.wide.region_3.11_spmd.sunk | while | flops 72364288 | bytes 25006472 | solution.py:151
  102.4 15.7 %while.28 = (s32[]{:T(128)}, f32[4,16,64]{2,1,0:T(8,128)S(1)}, f32[4,16,64]{2,1,0:T(8,128)S(1)}, f32[64,16,4,32]{0,3,2,1:T(8,128)S(1)}, f32[4,128]{1,0:T(4,128)S...) while((s32[]{:T(128)}, f32[4,16,64]{2,1,0:T(8,128)S(1)}, ...), condition=%wide.region_10.10_spmd, body=%wide.region_4.9_spmd.sunk | while | flops 72102144 | bytes 9457287 | solution.py:103
  129.0 15.7 %while.28 = (s32[]{:T(128)}, f32[4,16,64]{2,1,0:T(8,128)S(1)}, f32[4,16,64]{2,1,0:T(8,128)S(1)}, f32[64,16,4,32]{0,3,2,1:T(8,128)S(1)}, f32[4,128]{1,0:T(4,128)S...) while((s32[]{:T(128)}, f32[4,16,64]{2,1,0:T(8,128)S(1)}, ...), condition=%wide.region_10.10_spmd, body=%wide.region_4.9_spmd.sunk | while | flops 72102144 | bytes 9457287 | solution.py:103
  130.3 5.2 %conditional.2 = ((f32[4,16,64]{2,1,0:T(8,128)S(1)}, f32[4,16,64]{2,1,0:T(8,128)S(1)}, f32[64,16,4,32]{0,3,2,1:T(8,128)S(1)})) conditional(s32[]{:T(128)} %convert_element_type.93, (f32[4,16,64]{2,1,0:T(8,128)S(1)}, f32[4,16,64]{2,1,0:T(8,128)S(1)}, f32[64,16,4,32]{0,3,2,1:T(8,128)S(1)}) %tuple.72, (f32[1,128]{1,0:T(1,128)S(1)}, ...), branch_computations={%region_6.5_spmd, %region_7.8_spmd} | conditional | flops 72102016 | bytes 9456036 | solution.py:98
  155.5 15.7 %while.28 = (s32[]{:T(128)}, f32[4,16,64]{2,1,0:T(8,128)S(1)}, f32[4,16,64]{2,1,0:T(8,128)S(1)}, f32[64,16,4,32]{0,3,2,1:T(8,128)S(1)}, f32[4,128]{1,0:T(4,128)S...) while((s32[]{:T(128)}, f32[4,16,64]{2,1,0:T(8,128)S(1)}, ...), condition=%wide.region_10.10_spmd, body=%wide.region_4.9_spmd.sunk | while | flops 72102144 | bytes 9457287 | solution.py:103
  156.8 5.2 %conditional.2 = ((f32[4,16,64]{2,1,0:T(8,128)S(1)}, f32[4,16,64]{2,1,0:T(8,128)S(1)}, f32[64,16,4,32]{0,3,2,1:T(8,128)S(1)})) conditional(s32[]{:T(128)} %convert_element_type.93, (f32[4,16,64]{2,1,0:T(8,128)S(1)}, f32[4,16,64]{2,1,0:T(8,128)S(1)}, f32[64,16,4,32]{0,3,2,1:T(8,128)S(1)}) %tuple.72, (f32[1,128]{1,0:T(1,128)S(1)}, ...), branch_computations={%region_6.5_spmd, %region_7.8_spmd} | conditional | flops 72102016 | bytes 9456036 | solution.py:98
  164.7 5.2 %conditional.2 = ((f32[4,16,64]{2,1,0:T(8,128)S(1)}, f32[4,16,64]{2,1,0:T(8,128)S(1)}, f32[64,16,4,32]{0,3,2,1:T(8,128)S(1)})) conditional(s32[]{:T(128)} %convert_element_type.93, (f32[4,16,64]{2,1,0:T(8,128)S(1)}, f32[4,16,64]{2,1,0:T(8,128)S(1)}, f32[64,16,4,32]{0,3,2,1:T(8,128)S(1)}) %tuple.72, (f32[1,128]{1,0:T(1,128)S(1)}, ...), branch_computations={%region_6.5_spmd, %region_7.8_spmd} | conditional | flops 72102016 | bytes 9456036 | solution.py:98
  182.1 15.7 %while.28 = (s32[]{:T(128)}, f32[4,16,64]{2,1,0:T(8,128)S(1)}, f32[4,16,64]{2,1,0:T(8,128)S(1)}, f32[64,16,4,32]{0,3,2,1:T(8,128)S(1)}, f32[4,128]{1,0:T(4,128)S...) while((s32[]{:T(128)}, f32[4,16,64]{2,1,0:T(8,128)S(1)}, ...), condition=%wide.region_10.10_spmd, body=%wide.region_4.9_spmd.sunk | while | flops 72102144 | bytes 9457287 | solution.py:103
  183.4 5.2 %conditional.2 = ((f32[4,16,64]{2,1,0:T(8,128)S(1)}, f32[4,16,64]{2,1,0:T(8,128)S(1)}, f32[64,16,4,32]{0,3,2,1:T(8,128)S(1)})) conditional(s32[]{:T(128)} %convert_element_type.93, (f32[4,16,64]{2,1,0:T(8,128)S(1)}, f32[4,16,64]{2,1,0:T(8,128)S(1)}, f32[64,16,4,32]{0,3,2,1:T(8,128)S(1)}) %tuple.72, (f32[1,128]{1,0:T(1,128)S(1)}, ...), branch_computations={%region_6.5_spmd, %region_7.8_spmd} | conditional | flops 72102016 | bytes 9456036 | solution.py:98
  208.6 15.7 %while.28 = (s32[]{:T(128)}, f32[4,16,64]{2,1,0:T(8,128)S(1)}, f32[4,16,64]{2,1,0:T(8,128)S(1)}, f32[64,16,4,32]{0,3,2,1:T(8,128)S(1)}, f32[4,128]{1,0:T(4,128)S...) while((s32[]{:T(128)}, f32[4,16,64]{2,1,0:T(8,128)S(1)}, ...), condition=%wide.region_10.10_spmd, body=%wide.region_4.9_spmd.sunk | while | flops 72102144 | bytes 9457287 | solution.py:103
  217.8 5.2 %conditional.2 = ((f32[4,16,64]{2,1,0:T(8,128)S(1)}, f32[4,16,64]{2,1,0:T(8,128)S(1)}, f32[64,16,4,32]{0,3,2,1:T(8,128)S(1)})) conditional(s32[]{:T(128)} %convert_element_type.93, (f32[4,16,64]{2,1,0:T(8,128)S(1)}, f32[4,16,64]{2,1,0:T(8,128)S(1)}, f32[64,16,4,32]{0,3,2,1:T(8,128)S(1)}) %tuple.72, (f32[1,128]{1,0:T(1,128)S(1)}, ...), branch_computations={%region_6.5_spmd, %region_7.8_spmd} | conditional | flops 72102016 | bytes 9456036 | solution.py:98
  235.1 15.7 %while.28 = (s32[]{:T(128)}, f32[4,16,64]{2,1,0:T(8,128)S(1)}, f32[4,16,64]{2,1,0:T(8,128)S(1)}, f32[64,16,4,32]{0,3,2,1:T(8,128)S(1)}, f32[4,128]{1,0:T(4,128)S...) while((s32[]{:T(128)}, f32[4,16,64]{2,1,0:T(8,128)S(1)}, ...), condition=%wide.region_10.10_spmd, body=%wide.region_4.9_spmd.sunk | while | flops 72102144 | bytes 9457287 | solution.py:103
  261.7 15.7 %while.28 = (s32[]{:T(128)}, f32[4,16,64]{2,1,0:T(8,128)S(1)}, f32[4,16,64]{2,1,0:T(8,128)S(1)}, f32[64,16,4,32]{0,3,2,1:T(8,128)S(1)}, f32[4,128]{1,0:T(4,128)S...) while((s32[]{:T(128)}, f32[4,16,64]{2,1,0:T(8,128)S(1)}, ...), condition=%wide.region_10.10_spmd, body=%wide.region_4.9_spmd.sunk | while | flops 72102144 | bytes 9457287 | solution.py:103
  263.0 5.2 %conditional.2 = ((f32[4,16,64]{2,1,0:T(8,128)S(1)}, f32[4,16,64]{2,1,0:T(8,128)S(1)}, f32[64,16,4,32]{0,3,2,1:T(8,128)S(1)})) conditional(s32[]{:T(128)} %convert_element_type.93, (f32[4,16,64]{2,1,0:T(8,128)S(1)}, f32[4,16,64]{2,1,0:T(8,128)S(1)}, f32[64,16,4,32]{0,3,2,1:T(8,128)S(1)}) %tuple.72, (f32[1,128]{1,0:T(1,128)S(1)}, ...), branch_computations={%region_6.5_spmd, %region_7.8_spmd} | conditional | flops 72102016 | bytes 9456036 | solution.py:98
  288.2 15.7 %while.28 = (s32[]{:T(128)}, f32[4,16,64]{2,1,0:T(8,128)S(1)}, f32[4,16,64]{2,1,0:T(8,128)S(1)}, f32[64,16,4,32]{0,3,2,1:T(8,128)S(1)}, f32[4,128]{1,0:T(4,128)S...) while((s32[]{:T(128)}, f32[4,16,64]{2,1,0:T(8,128)S(1)}, ...), condition=%wide.region_10.10_spmd, body=%wide.region_4.9_spmd.sunk | while | flops 72102144 | bytes 9457287 | solution.py:103
  289.5 5.2 %conditional.2 = ((f32[4,16,64]{2,1,0:T(8,128)S(1)}, f32[4,16,64]{2,1,0:T(8,128)S(1)}, f32[64,16,4,32]{0,3,2,1:T(8,128)S(1)})) conditional(s32[]{:T(128)} %convert_element_type.93, (f32[4,16,64]{2,1,0:T(8,128)S(1)}, f32[4,16,64]{2,1,0:T(8,128)S(1)}, f32[64,16,4,32]{0,3,2,1:T(8,128)S(1)}) %tuple.72, (f32[1,128]{1,0:T(1,128)S(1)}, ...), branch_computations={%region_6.5_spmd, %region_7.8_spmd} | conditional | flops 72102016 | bytes 9456036 | solution.py:98
  310.8 11.1 %collective-permute-done = bf16[128,16,128]{2,1,0:T(8,128)(2,1)S(1)} collective-permute-done((bf16[128,16,128]{2,1,0:T(8,128)(2,1)S(1)}, bf16[128,16,128]{2,1,0:T(8,128)(2,1)S(1)}, u32[]{:S(2)}, u32[]{:S(2)}) %collective-permute-start) | collective-permute-done | bytes 524320 | tf_op jit(solution)/shard_map/ppermute | solution.py:30
  321.9 9.5 %collective-permute-done.1 = bf16[128,16,128]{2,1,0:T(8,128)(2,1)S(1)} collective-permute-done((bf16[128,16,128]{2,1,0:T(8,128)(2,1)S(1)}, bf16[128,16,128]{2,1,0:T(8,128)(2,1)S(1)}, u32[]{:S(2)}, u32[]{:S(2)}) %collective-permute-start.1) | collective-permute-done | bytes 524320 | tf_op jit(solution)/shard_map/ppermute | solution.py:30
  339.6 8.7 %fusion.20 = bf16[128,64,128]{2,0,1:T(8,128)(2,1)} fusion(f32[128,64]{0,1:T(8,128)S(1)} %broadcast_multiply_fusion, f32[128]{0:T(128)S(1)} %copy-done.11, bf16[128,64,128]{2,1,0:T(8,128)(2,1)S(1)} %copy-done.2, f32[128,64,128]{2,1,0:T(8,128)} %bitcast.109, bf16[128,64,128]{2,0,1:T(8,128)(2,1)} %copy-done.3, f32[128]{0:T(128)S(1)} %copy-done.12, ...), kind=kOutput, calls=%fused_computation.36 | convolution fusion | flops 548405248 | bytes 10585088 | tf_op jit(solution)/shard_map/dot_general | solution.py:158
  (382 shorter events, 286.8 us)
Async XLA Ops:
  6.5 333.1 %copy-start = (bf16[128,128]{1,0:T(8,128)(2,1)S(1)}, bf16[128,128]{1,0:T(8,128)(2,1)}, u32[]{:S(2)}) copy-start(bf16[128,128]{1,0:T(8,128)(2,1)} %param.21) | copy-start | bytes 98308
  6.5 3.6 copy-start.1
  6.5 9.7 %copy-start.9 = (f32[128]{0:T(128)S(1)}, f32[128]{0:T(128)}, u32[]{:S(2)}) copy-start(f32[128]{0:T(128)} %param.16) | copy-start | bytes 1540
  6.5 9.7 %copy-start.8 = (f32[128]{0:T(128)S(1)}, f32[128]{0:T(128)}, u32[]{:S(2)}) copy-start(f32[128]{0:T(128)} %param.17) | copy-start | bytes 1540
  6.5 80.9 %all-gather.2.cloned.1.call-start = ((), (), s32[]{:S(2)}) async-start(), calls=%async_computation.1 | async-start | bytes 4718592 | tf_op jit(solution)/shard_map/all_gather | solution.py:134
  16.3 6.3 %copy-start.7 = (bf16[128,4]{0,1:T(4,128)(2,1)S(1)}, bf16[128,4]{0,1:T(4,128)(2,1)}, u32[]{:S(2)}) copy-start(bf16[128,4]{0,1:T(4,128)(2,1)} %param.20) | copy-start | bytes 3076
  21.2 1.3 copy-start.3
  35.5 3.8 %copy-start.10 = (s32[4]{0:T(128)S(1)}, s32[4]{0:T(128)}, u32[]{:S(2)}) copy-start(s32[4]{0:T(128)} %param.23) | copy-start | bytes 52
  35.5 27.0 %all-to-all-start = ((bf16[128,64,128]{2,0,1:T(8,128)(2,1)}), bf16[128,64,128]{2,0,1:T(8,128)(2,1)S(1)}, u32[]{:S(2)}, u32[]{:S(2)}) async-start(bf16[128,64,128]{2,0,1:T(8,128)(2,1)} %copy-done.3), calls=%async_computation | async-start | bytes 4194304 | tf_op jit(solution)/shard_map/all_to_all | solution.py:123
  62.5 0.9 copy-start.6
  75.8 2.2 copy-start.4
  80.9 2.3 copy-start.5
  307.0 14.9 %collective-permute-start = (bf16[128,16,128]{2,1,0:T(8,128)(2,1)S(1)}, bf16[128,16,128]{2,1,0:T(8,128)(2,1)S(1)}, u32[]{:S(2)}, u32[]{:S(2)}) collective-permute-start(bf16[128,16,128]{2,1,0:T(8,128)(2,1)S(1)} %get-tuple-element.297), channel_id=1, source_target_pairs={{0,8},{8,0},{16,24},{24,16},{1,9},{9,1},{17,25},{25,17},{2,10},{10... | collective-permute-start | bytes 1572872 | tf_op jit(solution)/shard_map/ppermute | solution.py:30
  308.5 22.9 %collective-permute-start.1 = (bf16[128,16,128]{2,1,0:T(8,128)(2,1)S(1)}, bf16[128,16,128]{2,1,0:T(8,128)(2,1)S(1)}, u32[]{:S(2)}, u32[]{:S(2)}) collective-permute-start(bf16[128,16,128]{2,1,0:T(8,128)(2,1)S(1)} %get-tuple-element.296), channel_id=1, source_target_pairs={{0,16},{8,24},{16,0},{24,8},{1,17},{9,25},{17,1},{25,9},{2,18},{10... | collective-permute-start | bytes 1572872 | tf_op jit(solution)/shard_map/ppermute | solution.py:30
  309.0 22.4 %collective-permute-start.2 = (bf16[128,16,128]{2,1,0:T(8,128)(2,1)S(1)}, bf16[128,16,128]{2,1,0:T(8,128)(2,1)}, u32[]{:S(2)}, u32[]{:S(2)}) collective-permute-start(bf16[128,16,128]{2,1,0:T(8,128)(2,1)S(1)} %get-tuple-element.295), channel_id=1, source_target_pairs={{0,24},{8,16},{16,8},{24,0},{1,25},{9,17},{17,9},{25,1},{2,26},{10... | collective-permute-start | bytes 1572872 | tf_op jit(solution)/shard_map/ppermute | solution.py:30
  337.0 2.6 copy-start.2
  337.0 2.6 copy-start.11
  337.0 2.6 copy-start.12
Sparse Core Ops, SparseCore 0:
  35.6 47.1 all-gather.1
